TPU v7x, 32 devices: a whole 2x2x4 slice. The times are simulated.
32 devices in a mesh: shard: 2 (over x), replica: 16 (over z, y, core).
Axes of the slice: x: 2, y: 2, z: 4, core: 2. Of those that a mesh axis runs over, the one named last changes fastest.
Arguments:
- x_in: bfloat16 [32, 128, 2048], P(('shard', 'replica')), may hold values from -6 to 6
- cotangent: bfloat16 [32, 128, 2048], P(('shard', 'replica')), may hold values from -6 to 6
- w_query: bfloat16 [2048, 1024], P('shard'), may hold values from -0.088388348 to 0.088388348
- w_key: bfloat16 [2048, 1024], P('shard'), may hold values from -0.088388348 to 0.088388348
- w_value: bfloat16 [2048, 1024], P('shard'), may hold values from -0.125 to 0.125
- w_out: bfloat16 [1024, 2048], P('shard'), may hold values from -0.1875 to 0.1875
- w_gate: bfloat16 [2048, 4096], P('shard'), may hold values from -0.125 to 0.125
- w_up: bfloat16 [2048, 4096], P('shard'), may hold values from -0.125 to 0.125
- w_down: bfloat16 [4096, 2048], P('shard'), may hold values from -0.09375 to 0.09375
- gain_query: bfloat16 [1024], P('shard'), may hold values from 0.5 to 5
- gain_key: bfloat16 [1024], P('shard'), may hold values from 0.5 to 5
- gain_attn: bfloat16 [2048], P('shard'), may hold values from 0.5 to 1.5
- gain_mlp: bfloat16 [2048], P('shard'), may hold values from 0.5 to 1.5
Outputs:
- output: bfloat16 [32, 128, 2048], P(('shard', 'replica'))
- grad_input: float32 [32, 128, 2048], P(('shard', 'replica'))
- grad_w_query: float32 [2048, 1024], P(('shard', 'replica'))
- grad_w_key: float32 [2048, 1024], P(('shard', 'replica'))
- grad_w_value: float32 [2048, 1024], P(('shard', 'replica'))
- grad_w_out: float32 [1024, 2048], P(('shard', 'replica'))
- grad_w_gate: float32 [2048, 4096], P(('shard', 'replica'))
- grad_w_up: float32 [2048, 4096], P(('shard', 'replica'))
- grad_w_down: float32 [4096, 2048], P(('shard', 'replica'))
- grad_gain_query: float32 [1024], P(('shard', 'replica'))
- grad_gain_key: float32 [1024], P(('shard', 'replica'))
- grad_gain_attn: float32 [2048], P(('shard', 'replica'))
- grad_gain_mlp: float32 [2048], P(('shard', 'replica'))
All inputs are finite; a program needn't handle non-finite values.
Results may differ from a plain program's by a relative error of at most 0.018.
Values may be sent and summed in bfloat16 or wider, within the bound.
A program may use at most 512 MiB of HBM per device.

v0:
```python
import math
import jax
import jax.numpy as jnp
from jax import lax
from jax.sharding import PartitionSpec as P

HD = 128
eps_norm = 1e-06
rope_theta = 500000.0


def rope_tables(length, half):
    position = jnp.arange(length).astype(jnp.float32)[:, None]
    exponent = jnp.arange(half).astype(jnp.float32) * (1.0 / half)
    angle = position * rope_theta ** (-exponent)
    return (jnp.cos(angle), jnp.sin(angle))


def rotate(field, wave_cos, wave_sin):
    half = field.shape[-1] // 2
    first_half = field[..., :half]
    second_half = field[..., half:]
    cos_part = wave_cos[None, :, None, :]
    sin_part = wave_sin[None, :, None, :]
    return jnp.concatenate(
        [
            first_half * cos_part - second_half * sin_part,
            second_half * cos_part + first_half * sin_part,
        ],
        axis=-1,
    )


def unrotate(field, wave_cos, wave_sin):
    half = field.shape[-1] // 2
    first_half = field[..., :half]
    second_half = field[..., half:]
    cos_part = wave_cos[None, :, None, :]
    sin_part = wave_sin[None, :, None, :]
    return jnp.concatenate(
        [
            first_half * cos_part + second_half * sin_part,
            second_half * cos_part - first_half * sin_part,
        ],
        axis=-1,
    )


def rms_scale(field):
    return lax.rsqrt(jnp.mean(field * field, axis=-1, keepdims=True) + eps_norm)


def norm_back(grad_out, field, scale, gain):
    weighted = grad_out * gain
    inner = jnp.mean(weighted * field, axis=-1, keepdims=True)
    grad_field = scale * weighted - field * scale**3 * inner
    grad_gain = jnp.sum(grad_out * field * scale, axis=0)
    return (grad_field, grad_gain)


def matmul(left, right):
    return jnp.dot(left, right, preferred_element_type=jnp.float32)


def attn_scores(query_rot, key_rot, causal):
    scores = jnp.einsum(
        "sqhd,skhd->shqk", query_rot, key_rot, preferred_element_type=jnp.float32
    ) / math.sqrt(HD)
    return jnp.where(causal, scores, -jnp.inf)


def body(
    x_in,
    cotangent,
    w_query,
    w_key,
    w_value,
    w_out,
    w_gate,
    w_up,
    w_down,
    gain_query,
    gain_key,
    gain_attn,
    gain_mlp,
):
    attn_set = (
        lax.all_gather(w_query, "shard", axis=0, tiled=True),
        lax.all_gather(w_key, "shard", axis=0, tiled=True),
        lax.all_gather(w_value, "shard", axis=0, tiled=True),
        lax.all_gather(w_out, "shard", axis=0, tiled=True),
        lax.all_gather(gain_query, "shard", axis=0, tiled=True),
        lax.all_gather(gain_key, "shard", axis=0, tiled=True),
        lax.all_gather(gain_attn, "shard", axis=0, tiled=True),
    )
    mlp_set = (
        lax.all_gather(w_gate, "shard", axis=0, tiled=True),
        lax.all_gather(w_up, "shard", axis=0, tiled=True),
        lax.all_gather(w_down, "shard", axis=0, tiled=True),
        lax.all_gather(gain_mlp, "shard", axis=0, tiled=True),
    )
    seq_count, length, model_width = x_in.shape
    att_width = attn_set[0].shape[1]
    head_count = att_width // HD
    four_shape = (seq_count, length, head_count, HD)
    token_rows = x_in.reshape(seq_count * length, model_width)
    wave_cos, wave_sin = rope_tables(length, HD // 2)
    causal = jnp.arange(length)[:, None] >= jnp.arange(length)[None, :]
    query_proj = matmul(token_rows, attn_set[0])
    query_scale = rms_scale(query_proj)
    query_normed = query_proj * query_scale * attn_set[4].astype(jnp.float32)
    key_proj = matmul(token_rows, attn_set[1])
    key_scale = rms_scale(key_proj)
    key_normed = key_proj * key_scale * attn_set[5].astype(jnp.float32)
    value_four = matmul(token_rows, attn_set[2]).astype(jnp.bfloat16).reshape(four_shape)
    query_rot = rotate(query_normed.reshape(four_shape), wave_cos, wave_sin).astype(jnp.bfloat16)
    key_rot = rotate(key_normed.reshape(four_shape), wave_cos, wave_sin).astype(jnp.bfloat16)
    scores = attn_scores(query_rot, key_rot, causal)
    row_peak = jnp.max(scores, axis=-1, keepdims=True)
    log_total = row_peak + jnp.log(jnp.sum(jnp.exp(scores - row_peak), axis=-1, keepdims=True))
    probs_low = jnp.exp(scores - log_total).astype(jnp.bfloat16)
    attn_mixed = jnp.einsum(
        "shqk,skhd->sqhd", probs_low, value_four, preferred_element_type=jnp.float32
    )
    attn_mixed = attn_mixed.astype(jnp.bfloat16).reshape(-1, att_width)
    attn_proj = matmul(attn_mixed, attn_set[3])
    attn_scale = rms_scale(attn_proj)
    residual = token_rows.astype(jnp.float32) + attn_proj * attn_scale * attn_set[6].astype(
        jnp.float32
    )
    residual_low = residual.astype(jnp.bfloat16)
    gate_proj = matmul(residual_low, mlp_set[0])
    up_proj = matmul(residual_low, mlp_set[1])
    gate_sigmoid = jax.nn.sigmoid(gate_proj)
    gate_silu = gate_proj * gate_sigmoid
    hidden = (gate_silu * up_proj).astype(jnp.bfloat16)
    down_proj = matmul(hidden, mlp_set[2])
    down_scale = rms_scale(down_proj)
    output = residual + down_proj * down_scale * mlp_set[3].astype(jnp.float32)
    mlp_back = (
        lax.all_gather(w_gate, "shard", axis=0, tiled=True),
        lax.all_gather(w_up, "shard", axis=0, tiled=True),
        lax.all_gather(w_down, "shard", axis=0, tiled=True),
        lax.all_gather(gain_mlp, "shard", axis=0, tiled=True),
    )
    grad_output = cotangent.reshape(-1, model_width).astype(jnp.float32)
    grad_down, grad_gain_mlp = norm_back(
        grad_output, down_proj, down_scale, mlp_back[3].astype(jnp.float32)
    )
    grad_down = grad_down.astype(jnp.bfloat16)
    grad_w_down = matmul(hidden.T, grad_down)
    grad_hidden = matmul(grad_down, mlp_back[2].T)
    grad_gate = (
        grad_hidden * up_proj * gate_sigmoid * (1.0 + gate_proj * (1.0 - gate_sigmoid))
    ).astype(jnp.bfloat16)
    grad_up = (grad_hidden * gate_silu).astype(jnp.bfloat16)
    grad_w_gate = matmul(residual_low.T, grad_gate)
    grad_w_up = matmul(residual_low.T, grad_up)
    grad_residual = grad_output + matmul(grad_gate, mlp_back[0].T) + matmul(grad_up, mlp_back[1].T)
    mlp_grads = (grad_w_gate, grad_w_up, grad_w_down, grad_gain_mlp)
    mlp_half = (
        lax.psum_scatter(
            mlp_grads[0].astype(jnp.bfloat16), "shard", scatter_dimension=0, tiled=True
        ).astype(jnp.float32),
        lax.psum_scatter(
            mlp_grads[1].astype(jnp.bfloat16), "shard", scatter_dimension=0, tiled=True
        ).astype(jnp.float32),
        lax.psum_scatter(
            mlp_grads[2].astype(jnp.bfloat16), "shard", scatter_dimension=0, tiled=True
        ).astype(jnp.float32),
        lax.psum_scatter(
            mlp_grads[3].astype(jnp.bfloat16), "shard", scatter_dimension=0, tiled=True
        ).astype(jnp.float32),
    )
    mlp_owned = (
        lax.psum_scatter(mlp_half[0], "replica", scatter_dimension=0, tiled=True),
        lax.psum_scatter(mlp_half[1], "replica", scatter_dimension=0, tiled=True),
        lax.psum_scatter(mlp_half[2], "replica", scatter_dimension=0, tiled=True),
        lax.psum_scatter(mlp_half[3], "replica", scatter_dimension=0, tiled=True),
    )
    attn_back = (
        lax.all_gather(w_query, "shard", axis=0, tiled=True),
        lax.all_gather(w_key, "shard", axis=0, tiled=True),
        lax.all_gather(w_value, "shard", axis=0, tiled=True),
        lax.all_gather(w_out, "shard", axis=0, tiled=True),
        lax.all_gather(gain_query, "shard", axis=0, tiled=True),
        lax.all_gather(gain_key, "shard", axis=0, tiled=True),
        lax.all_gather(gain_attn, "shard", axis=0, tiled=True),
    )
    grad_attn, grad_gain_attn = norm_back(
        grad_residual, attn_proj, attn_scale, attn_back[6].astype(jnp.float32)
    )
    grad_attn = grad_attn.astype(jnp.bfloat16)
    grad_w_out = matmul(attn_mixed.T, grad_attn)
    grad_mixed = matmul(grad_attn, attn_back[3].T).astype(jnp.bfloat16).reshape(four_shape)
    probs_again = jnp.exp(attn_scores(query_rot, key_rot, causal) - log_total)
    grad_value = jnp.einsum(
        "shqk,sqhd->skhd",
        probs_again.astype(jnp.bfloat16),
        grad_mixed,
        preferred_element_type=jnp.float32,
    ).astype(jnp.bfloat16)
    grad_probs = jnp.einsum(
        "sqhd,skhd->shqk", grad_mixed, value_four, preferred_element_type=jnp.float32
    )
    grad_scores = probs_again * (
        grad_probs - jnp.sum(probs_again * grad_probs, axis=-1, keepdims=True)
    )
    grad_scores = (grad_scores / math.sqrt(HD)).astype(jnp.bfloat16)
    grad_qrot = jnp.einsum(
        "shqk,skhd->sqhd", grad_scores, key_rot, preferred_element_type=jnp.float32
    )
    grad_krot = jnp.einsum(
        "shqk,sqhd->skhd", grad_scores, query_rot, preferred_element_type=jnp.float32
    )
    grad_qnormed = unrotate(grad_qrot, wave_cos, wave_sin).reshape(-1, att_width)
    grad_knormed = unrotate(grad_krot, wave_cos, wave_sin).reshape(-1, att_width)
    grad_query, grad_gain_query = norm_back(
        grad_qnormed, query_proj, query_scale, attn_back[4].astype(jnp.float32)
    )
    grad_key, grad_gain_key = norm_back(
        grad_knormed, key_proj, key_scale, attn_back[5].astype(jnp.float32)
    )
    grad_query = grad_query.astype(jnp.bfloat16)
    grad_key = grad_key.astype(jnp.bfloat16)
    grad_value = grad_value.reshape(-1, att_width)
    grad_w_query = matmul(token_rows.T, grad_query)
    grad_w_key = matmul(token_rows.T, grad_key)
    grad_w_value = matmul(token_rows.T, grad_value)
    grad_input = (
        grad_residual
        + matmul(grad_query, attn_back[0].T)
        + matmul(grad_key, attn_back[1].T)
        + matmul(grad_value, attn_back[2].T)
    )
    attn_grads = (
        grad_w_query,
        grad_w_key,
        grad_w_value,
        grad_w_out,
        grad_gain_query,
        grad_gain_key,
        grad_gain_attn,
    )
    attn_half = (
        lax.psum_scatter(
            attn_grads[0].astype(jnp.bfloat16), "shard", scatter_dimension=0, tiled=True
        ).astype(jnp.float32),
        lax.psum_scatter(
            attn_grads[1].astype(jnp.bfloat16), "shard", scatter_dimension=0, tiled=True
        ).astype(jnp.float32),
        lax.psum_scatter(
            attn_grads[2].astype(jnp.bfloat16), "shard", scatter_dimension=0, tiled=True
        ).astype(jnp.float32),
        lax.psum_scatter(
            attn_grads[3].astype(jnp.bfloat16), "shard", scatter_dimension=0, tiled=True
        ).astype(jnp.float32),
        lax.psum_scatter(
            attn_grads[4].astype(jnp.bfloat16), "shard", scatter_dimension=0, tiled=True
        ).astype(jnp.float32),
        lax.psum_scatter(
            attn_grads[5].astype(jnp.bfloat16), "shard", scatter_dimension=0, tiled=True
        ).astype(jnp.float32),
        lax.psum_scatter(
            attn_grads[6].astype(jnp.bfloat16), "shard", scatter_dimension=0, tiled=True
        ).astype(jnp.float32),
    )
    attn_owned = (
        lax.psum_scatter(attn_half[0], "replica", scatter_dimension=0, tiled=True),
        lax.psum_scatter(attn_half[1], "replica", scatter_dimension=0, tiled=True),
        lax.psum_scatter(attn_half[2], "replica", scatter_dimension=0, tiled=True),
        lax.psum_scatter(attn_half[3], "replica", scatter_dimension=0, tiled=True),
        lax.psum_scatter(attn_half[4], "replica", scatter_dimension=0, tiled=True),
        lax.psum_scatter(attn_half[5], "replica", scatter_dimension=0, tiled=True),
        lax.psum_scatter(attn_half[6], "replica", scatter_dimension=0, tiled=True),
    )
    return (
        output.astype(jnp.bfloat16).reshape(x_in.shape),
        grad_input.reshape(x_in.shape),
        attn_owned[0],
        attn_owned[1],
        attn_owned[2],
        attn_owned[3],
        mlp_owned[0],
        mlp_owned[1],
        mlp_owned[2],
        attn_owned[4],
        attn_owned[5],
        attn_owned[6],
        mlp_owned[3],
    )


def solution(mesh):
    return jax.shard_map(
        body,
        mesh=mesh,
        in_specs=(
            P(("shard", "replica"), None, None),
            P(("shard", "replica"), None, None),
            P("shard", None),
            P("shard", None),
            P("shard", None),
            P("shard", None),
            P("shard", None),
            P("shard", None),
            P("shard", None),
            P("shard"),
            P("shard"),
            P("shard"),
            P("shard"),
        ),
        out_specs=(
            P(("shard", "replica"), None, None),
            P(("shard", "replica"), None, None),
            P(("shard", "replica"), None),
            P(("shard", "replica"), None),
            P(("shard", "replica"), None),
            P(("shard", "replica"), None),
            P(("shard", "replica"), None),
            P(("shard", "replica"), None),
            P(("shard", "replica"), None),
            P(("shard", "replica")),
            P(("shard", "replica")),
            P(("shard", "replica")),
            P(("shard", "replica")),
        ),
        check_vma=False,
    )
```

profile of v0, /device:TPU:0, one launch (start us, length us, event | category | flops | bytes accessed | tf_op | source)
XLA Modules:
  0.0 2560.4 jit_solution(11630051221962567769)
XLA Ops:
  12.0 5.3 all-gather.1
  17.3 4.4 all-gather
  21.7 4.5 all_gather.50
  26.2 4.5 all_gather.54
  31.1 37.9 %all-gather.14.cloned.1.call-done = bf16[2048,1024]{1,0:T(8,128)(2,1)} async-done(((bf16[1024,1024]{1,0:T(8,128)(2,1)}), bf16[2048,1024]{1,0:T(8,128)(2,1)}) %all-gather.14.cloned.1.call-update) | async-done | bytes 4194320 | tf_op jit(solution)/shard_map/all_gather | solution.py:89
  69.1 3.0 multiply_reduce_fusion.7
  73.1 54.3 %all-gather.12.cloned.1.call-done = bf16[2048,1024]{1,0:T(8,128)(2,1)} async-done(((bf16[1024,1024]{1,0:T(8,128)(2,1)}), bf16[2048,1024]{1,0:T(8,128)(2,1)}) %all-gather.12.cloned.1.call-update) | async-done | bytes 4194320 | tf_op jit(solution)/shard_map/all_gather | solution.py:88
  133.5 52.2 %all-gather.10.cloned.1.call-done = bf16[2048,1024]{1,0:T(8,128)(2,1)} async-done(((bf16[1024,1024]{1,0:T(8,128)(2,1)}), bf16[2048,1024]{1,0:T(8,128)(2,1)}) %all-gather.10.cloned.1.call-update) | async-done | bytes 4194320 | tf_op jit(solution)/shard_map/all_gather | solution.py:90
  188.9 54.9 %all-gather.16.cloned.1.call-done = bf16[1024,2048]{1,0:T(8,128)(2,1)} async-done(((bf16[512,2048]{1,0:T(8,128)(2,1)}), bf16[1024,2048]{1,0:T(8,128)(2,1)}) %all-gather.16.cloned.1.call-update) | async-done | bytes 4194320 | tf_op jit(solution)/shard_map/all_gather | solution.py:91
  243.9 3.0 multiply_reduce_fusion.3
  247.1 197.0 %all-gather.18.cloned.1.call-done = bf16[2048,4096]{1,0:T(8,128)(2,1)} async-done(((bf16[1024,4096]{1,0:T(8,128)(2,1)}), bf16[2048,4096]{1,0:T(8,128)(2,1)}) %all-gather.18.cloned.1.call-update) | async-done | bytes 16777232 | tf_op jit(solution)/shard_map/all_gather | solution.py:97
  444.1 9.4 fusion.64
  453.5 190.8 %all-gather.20.cloned.1.call-done = bf16[2048,4096]{1,0:T(8,128)(2,1)} async-done(((bf16[1024,4096]{1,0:T(8,128)(2,1)}), bf16[2048,4096]{1,0:T(8,128)(2,1)}) %all-gather.20.cloned.1.call-update) | async-done | bytes 16777232 | tf_op jit(solution)/shard_map/all_gather | solution.py:98
  644.4 11.3 multiply_convert_fusion.2
  655.6 189.2 %all-gather.22.cloned.1.call-done = bf16[4096,2048]{1,0:T(8,128)(2,1)} async-done(((bf16[2048,2048]{1,0:T(8,128)(2,1)}), bf16[4096,2048]{1,0:T(8,128)(2,1)}) %all-gather.22.cloned.1.call-update) | async-done | bytes 16777232 | tf_op jit(solution)/shard_map/all_gather | solution.py:99
  844.8 8.9 multiply_reduce_fusion.2
  854.7 14.4 multiply_convert_fusion
  869.1 12.7 convolution_add_fusion.4
  881.8 13.7 multiply_reduce_fusion
  901.7 3.2 convert_bitcast_fusion
  916.1 3.3 convert_bitcast_fusion.1
  919.5 3.2 convolution_convert_fusion.3
  926.5 3.2 convert_bitcast_fusion.2
  930.7 8.5 convolution_convert_fusion
  940.5 8.1 convolution_convert_fusion.2
  949.8 8.1 convolution_convert_fusion.1
  959.5 4.2 copy.80
  963.8 52.5 %reduce-scatter.23.cloned.1.call-done = bf16[1024,1024]{0,1:T(8,128)(2,1)} async-done(((bf16[2048,1024]{0,1:T(8,128)(2,1)}), bf16[1024,1024]{0,1:T(8,128)(2,1)}) %reduce-scatter.23.cloned.1.call-update) | async-done | bytes 2097168 | tf_op jit(solution)/shard_map/reduce_scatter | solution.py:249
  1016.2 4.2 copy.78
  1020.5 52.3 %reduce-scatter.27.cloned.1.call-done = bf16[512,2048]{1,0:T(8,128)(2,1)} async-done(((bf16[1024,2048]{1,0:T(8,128)(2,1)}), bf16[512,2048]{1,0:T(8,128)(2,1)}) %reduce-scatter.27.cloned.1.call-update) | async-done | bytes 2097168 | tf_op jit(solution)/shard_map/reduce_scatter | solution.py:255
  1072.8 4.1 convert_element_type.282
  1077.0 52.5 %reduce-scatter.21.cloned.1.call-done = bf16[1024,1024]{0,1:T(8,128)(2,1)} async-done(((bf16[2048,1024]{0,1:T(8,128)(2,1)}), bf16[1024,1024]{0,1:T(8,128)(2,1)}) %reduce-scatter.21.cloned.1.call-update) | async-done | bytes 2097168 | tf_op jit(solution)/shard_map/reduce_scatter | solution.py:246
  1129.5 4.1 copy.76
  1133.7 187.2 %reduce-scatter.39.cloned.1.call-done = bf16[2048,2048]{1,0:T(8,128)(2,1)} async-done(((bf16[4096,2048]{1,0:T(8,128)(2,1)}), bf16[2048,2048]{1,0:T(8,128)(2,1)}) %reduce-scatter.39.cloned.1.call-update) | async-done | bytes 8388624 | tf_op jit(solution)/shard_map/reduce_scatter | solution.py:168
  1320.9 11.8 convert_element_type.288
  1332.7 179.7 %reduce-scatter.31.cloned.1.call-done = bf16[1024,4096]{1,0:T(8,128)(2,1)} async-done(((bf16[2048,4096]{1,0:T(8,128)(2,1)}), bf16[1024,4096]{1,0:T(8,128)(2,1)}) %reduce-scatter.31.cloned.1.call-update) | async-done | bytes 8388624 | tf_op jit(solution)/shard_map/reduce_scatter | solution.py:162
  1512.4 11.9 convert_element_type.284
  1524.6 179.2 %reduce-scatter.35.cloned.1.call-done = bf16[1024,4096]{1,0:T(8,128)(2,1)} async-done(((bf16[2048,4096]{1,0:T(8,128)(2,1)}), bf16[1024,4096]{1,0:T(8,128)(2,1)}) %reduce-scatter.35.cloned.1.call-update) | async-done | bytes 8388624 | tf_op jit(solution)/shard_map/reduce_scatter | solution.py:165
  1703.8 11.6 convert_element_type.286
  1719.9 6.8 all-reduce.9
  1726.8 59.8 %all-reduce.8 = (f32[512]{0:T(512)S(1)}, f32[512]{0:T(512)S(1)}, f32[1024]{0:T(1024)S(1)}, f32[1024]{0:T(1024)S(1)}) all-reduce(f32[512]{0:T(512)S(1)} %dynamic-slice_convert_fusion.3, f32[512]{0:T(512)S(1)} %dynamic-slice_convert_fusion.2, ...), channel_id=17, replica_groups=mesh['shard'=2,'replica'=16] {'replica'}, use_global_device_ids=true, to_apply=%region_27.28.clone | all-reduce | flops 3072 | bytes 24576
  1788.9 3.9 convolution_add_fusion.2
  1797.7 59.8 %reduce-scatter.45.cloned.1.call-done = f32[64,1024]{1,0:T(8,128)} async-done(((f32[1024,1024]{1,0:T(8,128)}), f32[64,1024]{1,0:T(8,128)}) %reduce-scatter.45.cloned.1.call-update) | async-done | bytes 262160
  1857.6 76.2 %reduce-scatter.29.cloned.1.call-done = f32[32,2048]{1,0:T(8,128)} async-done(((f32[512,2048]{1,0:T(8,128)}), f32[32,2048]{1,0:T(8,128)}) %reduce-scatter.29.cloned.1.call-update) | async-done | bytes 262160 | tf_op jit(solution)/shard_map/reduce_scatter | solution.py:272
  1933.7 76.1 %reduce-scatter.43.cloned.1.call-done = f32[64,1024]{1,0:T(8,128)} async-done(((f32[1024,1024]{1,0:T(8,128)}), f32[64,1024]{1,0:T(8,128)}) %reduce-scatter.43.cloned.1.call-update) | async-done | bytes 262160
  2009.9 181.1 %reduce-scatter.41.cloned.1.call-done = f32[128,2048]{1,0:T(8,128)} async-done(((f32[2048,2048]{1,0:T(8,128)}), f32[128,2048]{1,0:T(8,128)}) %reduce-scatter.41.cloned.1.call-update) | async-done | bytes 1048592 | tf_op jit(solution)/shard_map/reduce_scatter | solution.py:178
  2191.0 181.0 %reduce-scatter.33.cloned.1.call-done = f32[64,4096]{1,0:T(8,128)} async-done(((f32[1024,4096]{1,0:T(8,128)}), f32[64,4096]{1,0:T(8,128)}) %reduce-scatter.33.cloned.1.call-update) | async-done | bytes 1048592 | tf_op jit(solution)/shard_map/reduce_scatter | solution.py:176
  2372.0 181.1 %reduce-scatter.37.cloned.1.call-done = f32[64,4096]{1,0:T(8,128)} async-done(((f32[1024,4096]{1,0:T(8,128)}), f32[64,4096]{1,0:T(8,128)}) %reduce-scatter.37.cloned.1.call-update) | async-done | bytes 1048592 | tf_op jit(solution)/shard_map/reduce_scatter | solution.py:177
  (208 shorter events, 52.1 us)
Async XLA Ops:
  7.2 61.9 %all-gather.14.cloned.1.call-start = ((), (), s32[]{:S(2)}) async-start(), calls=%async_computation.16 | async-start | bytes 6291456 | tf_op jit(solution)/shard_map/all_gather | solution.py:89
  7.9 119.5 %all-gather.12.cloned.1.call-start = ((), (), s32[]{:S(2)}) async-start(), calls=%async_computation.15 | async-start | bytes 6291456 | tf_op jit(solution)/shard_map/all_gather | solution.py:88
  8.7 177.0 %all-gather.10.cloned.1.call-start = ((), (), s32[]{:S(2)}) async-start(), calls=%async_computation.14 | async-start | bytes 6291456 | tf_op jit(solution)/shard_map/all_gather | solution.py:90
  9.4 234.5 %all-gather.16.cloned.1.call-start = ((), (), s32[]{:S(2)}) async-start(), calls=%async_computation.17 | async-start | bytes 6291456 | tf_op jit(solution)/shard_map/all_gather | solution.py:91
  10.0 434.1 %all-gather.18.cloned.1.call-start = ((), (), s32[]{:S(2)}) async-start(), calls=%async_computation.18 | async-start | bytes 25165824 | tf_op jit(solution)/shard_map/all_gather | solution.py:97
  10.6 633.8 %all-gather.20.cloned.1.call-start = ((), (), s32[]{:S(2)}) async-start(), calls=%async_computation.19 | async-start | bytes 25165824 | tf_op jit(solution)/shard_map/all_gather | solution.py:98
  11.2 6.2 copy-start.43
  11.2 10.5 copy-start.40
  11.2 15.1 copy-start.41
  11.2 57.9 %copy-start = (bf16[1,128,2048]{2,1,0:T(8,128)(2,1)S(1)}, bf16[1,128,2048]{2,1,0:T(8,128)(2,1)}, u32[]{:S(2)}) copy-start(bf16[1,128,2048]{2,1,0:T(8,128)(2,1)} %param.13) | copy-start | bytes 1572868
  11.2 833.6 %all-gather.22.cloned.1.call-start = ((), (), s32[]{:S(2)}) async-start(), calls=%async_computation.20 | async-start | bytes 25165824 | tf_op jit(solution)/shard_map/all_gather | solution.py:99
  11.9 947.6 %reduce-scatter.25.cloned.1.call-start = ((), (), s32[]{:S(2)}) async-start(), calls=%async_computation.23 | async-start | bytes 6291456 | tf_op jit(solution)/shard_map/reduce_scatter | solution.py:252
  72.6 57.7 %copy-start.36 = (f32[128]{0:T(128)}, f32[128]{0:T(128)S(1)}, u32[]{:S(2)}) copy-start(f32[128]{0:T(128)S(1)} %get-tuple-element.78) | copy-start | bytes 1540
  133.4 110.5 %copy-start.5 = (f32[8,128,128]{1,2,0:T(8,128)}, f32[8,128,128]{1,2,0:T(8,128)S(1)}, u32[]{:S(2)}) copy-start(f32[8,128,128]{1,2,0:T(8,128)S(1)} %get-tuple-element.90) | copy-start | bytes 1572868
  133.5 113.4 %copy-start.31 = (f32[8,128]{1,0:T(8,128)}, f32[8,128]{1,0:T(8,128)S(1)}, u32[]{:S(2)}) copy-start(f32[8,128]{1,0:T(8,128)S(1)} %log_add_fusion) | copy-start | bytes 12292
  188.6 55.2 %copy-start.24 = (bf16[16,8,8,128]{3,2,1,0:T(8,128)(2,1)}, bf16[16,8,8,128]{3,2,1,0:T(8,128)(2,1)S(1)}, u32[]{:S(2)}) copy-start(bf16[16,8,8,128]{3,2,1,0:T(8,128)(2,1)S(1)} %fusion.10) | copy-start | bytes 786436
  188.9 264.6 %copy-start.22 = (bf16[8,128,128]{2,1,0:T(8,128)(2,1)}, bf16[8,128,128]{2,1,0:T(8,128)(2,1)S(1)}, u32[]{:S(2)}) copy-start(bf16[8,128,128]{2,1,0:T(8,128)(2,1)S(1)} %convolution_convert_fusion.5) | copy-start | bytes 786436
  844.8 9.0 copy-start.14
  853.8 15.3 copy-start.46
  853.8 41.8 %copy-start.38 = (f32[128]{0:T(128)}, f32[128]{0:T(128)S(1)}, u32[]{:S(2)}) copy-start(f32[128]{0:T(128)S(1)} %get-tuple-element.84) | copy-start | bytes 1540
  854.7 14.4 copy-start.48
  895.5 3.5 copy-start.3
  905.0 111.2 %reduce-scatter.23.cloned.1.call-start = ((), (), s32[]{:S(2)}) async-start(), calls=%async_computation.22 | async-start | bytes 6291456 | tf_op jit(solution)/shard_map/reduce_scatter | solution.py:249
  908.8 6.2 copy-start.10
  911.5 3.5 copy-start.37
  911.5 3.7 copy-start.45
  919.4 153.4 %reduce-scatter.27.cloned.1.call-start = ((), (), s32[]{:S(2)}) async-start(), calls=%async_computation.24 | async-start | bytes 6291456 | tf_op jit(solution)/shard_map/reduce_scatter | solution.py:255
  922.8 206.8 %reduce-scatter.21.cloned.1.call-start = ((), (), s32[]{:S(2)}) async-start(), calls=%async_computation.21 | async-start | bytes 6291456 | tf_op jit(solution)/shard_map/reduce_scatter | solution.py:246
  926.4 3.6 copy-start.11
  926.4 3.6 copy-start.39
  926.4 3.6 copy-start.47
  926.4 3.6 copy-start.49
  929.7 391.2 %reduce-scatter.39.cloned.1.call-start = ((), (), s32[]{:S(2)}) async-start(), calls=%async_computation.30 | async-start | bytes 25165824 | tf_op jit(solution)/shard_map/reduce_scatter | solution.py:168
  939.3 573.1 %reduce-scatter.31.cloned.1.call-start = ((), (), s32[]{:S(2)}) async-start(), calls=%async_computation.26 | async-start | bytes 25165824 | tf_op jit(solution)/shard_map/reduce_scatter | solution.py:162
  948.6 755.1 %reduce-scatter.35.cloned.1.call-start = ((), (), s32[]{:S(2)}) async-start(), calls=%async_computation.28 | async-start | bytes 25165824 | tf_op jit(solution)/shard_map/reduce_scatter | solution.py:165
  958.0 839.8 %reduce-scatter.47.cloned.1.call-start = ((), (), s32[]{:S(2)}) async-start(), calls=%async_computation.34 | async-start | bytes 4456448
  963.7 893.8 %reduce-scatter.45.cloned.1.call-start = ((), (), s32[]{:S(2)}) async-start(), calls=%async_computation.33 | async-start | bytes 4456448
  1020.4 913.3 %reduce-scatter.29.cloned.1.call-start = ((), (), s32[]{:S(2)}) async-start(), calls=%async_computation.25 | async-start | bytes 4456448 | tf_op jit(solution)/shard_map/reduce_scatter | solution.py:272
  1076.9 932.9 %reduce-scatter.43.cloned.1.call-start = ((), (), s32[]{:S(2)}) async-start(), calls=%async_computation.32 | async-start | bytes 4456448
  1133.7 1057.3 %reduce-scatter.41.cloned.1.call-start = ((), (), s32[]{:S(2)}) async-start(), calls=%async_computation.31 | async-start | bytes 17825792 | tf_op jit(solution)/shard_map/reduce_scatter | solution.py:178
  1332.7 1039.3 %reduce-scatter.33.cloned.1.call-start = ((), (), s32[]{:S(2)}) async-start(), calls=%async_computation.27 | async-start | bytes 17825792 | tf_op jit(solution)/shard_map/reduce_scatter | solution.py:176
  1524.3 1028.8 %reduce-scatter.37.cloned.1.call-start = ((), (), s32[]{:S(2)}) async-start(), calls=%async_computation.29 | async-start | bytes 17825792 | tf_op jit(solution)/shard_map/reduce_scatter | solution.py:177
  1715.4 4.4 copy-start.32
  1715.4 4.4 copy-start.33
  1715.4 73.5 %copy-start.4 = (f32[128,2048]{1,0:T(8,128)S(1)}, f32[128,2048]{1,0:T(8,128)}, u32[]{:S(2)}) copy-start(f32[128,2048]{1,0:T(8,128)} %get-tuple-element.97) | copy-start | bytes 3145732
  1715.4 73.5 %copy-start.21 = (bf16[128,1024]{1,0:T(8,128)(2,1)S(1)}, bf16[128,1024]{1,0:T(8,128)(2,1)}, u32[]{:S(2)}) copy-start(bf16[128,1024]{1,0:T(8,128)(2,1)} %copy-done.20) | copy-start | bytes 786436
  1715.4 77.3 %copy-start.19 = (bf16[128,1024]{1,0:T(8,128)(2,1)S(1)}, bf16[128,1024]{1,0:T(8,128)(2,1)}, u32[]{:S(2)}) copy-start(bf16[128,1024]{1,0:T(8,128)(2,1)} %copy-done.18) | copy-start | bytes 786436
  1786.6 6.2 copy-start.1
  (25 other events, 40.8 us)
Sparse Core Ops, SparseCore 0:
  9.5 59.4 all-gather.13
  70.6 56.7 all-gather.11
  128.9 56.7 all-gather.9
  187.1 56.7 all-gather.15
  245.2 198.8 all-gather.17
  445.5 198.8 all-gather.19
  645.9 198.8 all-gather.21
  905.1 54.3 reduce-scatter.24
  961.8 54.3 reduce-scatter.22
  1018.4 54.3 reduce-scatter.26
  1075.1 54.3 reduce-scatter.20
  1131.7 189.2 reduce-scatter.38
  1323.2 189.1 reduce-scatter.30
  1514.6 189.1 reduce-scatter.34
  1708.1 73.2 reduce-scatter.46
  1785.7 71.8 reduce-scatter.44
  1861.8 71.8 reduce-scatter.28
  1938.0 71.8 reduce-scatter.42
  2014.5 176.4 reduce-scatter.40
  2195.5 176.4 reduce-scatter.32
  2376.7 176.4 reduce-scatter.36
where the time goes:
time: 2570 us; the launch traced here: 2560 us
  waiting for transfers between devices  2240 us (87%)
  matrix products  138 us (5%)
  blocking collectives  85.3 us (3%)
  other arithmetic  50.8 us (2%)
  local copies, waits for them, and re-layouts  26.2 us (1%)
    all_gather x1, waiting for transfers between devices, body(): lax.all_gather(w_gate, 'shard', axis=0, tiled=True)  197 us
    all_gather x1, waiting for transfers between devices, body(): lax.all_gather(w_up, 'shard', axis=0, tiled=True)  191 us
    all_gather x1, waiting for transfers between devices, body(): lax.all_gather(w_down, 'shard', axis=0, tiled=True)  189 us
    reduce_scatter x1, waiting for transfers between devices, body(): lax.psum_scatter(mlp_grads[2].astype(jnp.bfloat16), 'shard', scatter_dime...  187 us
    reduce_scatter x1, waiting for transfers between devices, body(): lax.psum_scatter(mlp_half[1], 'replica', scatter_dimension=0, tiled=True)  181 us
    reduce_scatter x1, waiting for transfers between devices, body(): lax.psum_scatter(mlp_half[2], 'replica', scatter_dimension=0, tiled=True)  181 us
    reduce_scatter x1, waiting for transfers between devices, body(): lax.psum_scatter(mlp_half[0], 'replica', scatter_dimension=0, tiled=True)  181 us
    reduce_scatter x1, waiting for transfers between devices, body(): lax.psum_scatter(mlp_grads[0].astype(jnp.bfloat16), 'shard', scatter_dime...  180 us
  transfers between devices with their start and end apart: 21, of which 20 were waited for; matrix products, arithmetic and copies ran while one was open for 6% of the time, Pallas kernels for 0%

commit v1 on v0

--- a/solution.py
+++ b/solution.py
@@ -7,6 +7,19 @@
 HD = 128
 eps_norm = 1e-06
 rope_theta = 500000.0
+
+
+def form_the_skins(vector):
+    v1 = lax.axis_size("shard")
+    outcome_arr, out_arr = (v1, lax.axis_index("shard"))
+    e_next, answer = (vector, 1)
+    while answer < outcome_arr:
+        parts_out = lax.ppermute(e_next, "shard", [(k, k ^ answer) for k in range(outcome_arr)])
+        mat_out = jnp.concatenate([e_next, parts_out], axis=0)
+        q_next = jnp.concatenate([parts_out, e_next], axis=0)
+        e_next = jnp.where(out_arr & answer == 0, mat_out, q_next)
+        answer = 2 * answer
+    return e_next
 
 
 def rope_tables(length, half):
@@ -95,7 +108,7 @@
     )
     mlp_set = (
         lax.all_gather(w_gate, "shard", axis=0, tiled=True),
-        lax.all_gather(w_up, "shard", axis=0, tiled=True),
+        form_the_skins(w_up),
         lax.all_gather(w_down, "shard", axis=0, tiled=True),
         lax.all_gather(gain_mlp, "shard", axis=0, tiled=True),
     )

time: 2570 us -> 2670 us (1.039)
  blocking collectives: 85.3 us -> 396 us
  waiting for transfers between devices: 2240 us -> 2010 us
    all_gather x1, blocking collectives: 5.29 us -> 316 us  [body(): lax.all_gather(gain_key, 'shard', axis=0, tiled=True)]
    all_gather x1, waiting for transfers between devices: 54.3 us -> 0.02 us  [body(): lax.all_gather(w_query, 'shard', axis=0, tiled=True)]
    all_gather x1, waiting for transfers between devices: 52.2 us -> 0.02 us  [body(): lax.all_gather(w_value, 'shard', axis=0, tiled=True)]
    all_gather x1, waiting for transfers between devices: 37.9 us -> 0.02 us  [body(): lax.all_gather(w_key, 'shard', axis=0, tiled=True)]
    all_gather x1, waiting for transfers between devices: 54.9 us -> 21 us  [body(): lax.all_gather(w_out, 'shard', axis=0, tiled=True)]
    all_gather x1, waiting for transfers between devices: 191 us -> 159 us  [body(): lax.all_gather(w_up, 'shard', axis=0, tiled=True)]
  transfers between devices with their start and end apart: 21 -> 22, of which waited for: 20 -> 17; matrix products, arithmetic and copies ran while one was open for 6% -> 7% of each run, Pallas kernels for 0% -> 0%
where the time goes in v1:
time: 2670 us; the launch traced here: 2660 us
  waiting for transfers between devices  2010 us (75%)
  blocking collectives  396 us (15%)
  matrix products  150 us (6%)
  other arithmetic  50.8 us (2%)
  local copies, waits for them, and re-layouts  27.3 us (1%)
    all_gather x1, blocking collectives, body(): lax.all_gather(gain_key, 'shard', axis=0, tiled=True)  316 us
    all_gather x1, waiting for transfers between devices, body(): lax.all_gather(w_gate, 'shard', axis=0, tiled=True)  197 us
    reduce_scatter x1, waiting for transfers between devices, body(): lax.psum_scatter(mlp_grads[2].astype(jnp.bfloat16), 'shard', scatter_dime...  187 us
    reduce_scatter x1, waiting for transfers between devices, body(): lax.psum_scatter(mlp_half[1], 'replica', scatter_dimension=0, tiled=True)  181 us
    reduce_scatter x1, waiting for transfers between devices, body(): lax.psum_scatter(mlp_half[2], 'replica', scatter_dimension=0, tiled=True)  181 us
    reduce_scatter x1, waiting for transfers between devices, body(): lax.psum_scatter(mlp_half[0], 'replica', scatter_dimension=0, tiled=True)  181 us
    reduce_scatter x1, waiting for transfers between devices, body(): lax.psum_scatter(mlp_grads[0].astype(jnp.bfloat16), 'shard', scatter_dime...  180 us
    reduce_scatter x1, waiting for transfers between devices, body(): lax.psum_scatter(mlp_grads[1].astype(jnp.bfloat16), 'shard', scatter_dime...  179 us
  transfers between devices with their start and end apart: 22, of which 17 were waited for; matrix products, arithmetic and copies ran while one was open for 7% of the time, Pallas kernels for 0%

profile of v1, /device:TPU:0, one launch (start us, length us, event | category | flops | bytes accessed | tf_op | source)
XLA Modules:
  0.0 2658.3 jit_solution(11696989344610504211)
XLA Ops:
  12.0 3.0 collective-permute-start
  15.0 315.6 %all-gather.1 = bf16[2,1,512]{2,1,0:T(2,128)(2,1)S(1)} all-gather(bf16[1,1,512]{2,1,0:T(2,128)(2,1)S(1)} %reshape.315), channel_id=1, replica_groups=mesh['shard'=2,'replica'=16] {'shard'}, dimensions={0}, use_global_device_ids=true | all-gather | bytes 3072 | tf_op jit(solution)/shard_map/all_gather | solution.py:106
  330.7 4.4 all-gather
  335.1 4.5 all_gather.49
  339.6 4.5 all_gather.52
  344.6 3.0 multiply_reduce_fusion.7
  348.6 3.0 multiply_reduce_fusion.8
  358.0 21.0 all-gather.16.cloned.1.call-done
  379.0 3.0 multiply_reduce_fusion.3
  382.3 197.0 %all-gather.18.cloned.1.call-done = bf16[2048,4096]{1,0:T(8,128)(2,1)} async-done(((bf16[1024,4096]{1,0:T(8,128)(2,1)}), bf16[2048,4096]{1,0:T(8,128)(2,1)}) %all-gather.18.cloned.1.call-update) | async-done | bytes 16777232 | tf_op jit(solution)/shard_map/all_gather | solution.py:110
  579.3 8.1 fusion.72
  588.8 20.2 multiply_convert_fusion.2
  609.0 170.6 %all-gather.20.cloned.1.call-done = bf16[4096,2048]{1,0:T(8,128)(2,1)} async-done(((bf16[2048,2048]{1,0:T(8,128)(2,1)}), bf16[4096,2048]{1,0:T(8,128)(2,1)}) %all-gather.20.cloned.1.call-update) | async-done | bytes 16777232 | tf_op jit(solution)/shard_map/all_gather | solution.py:112
  779.5 8.6 multiply_reduce_fusion.2
  789.1 18.7 multiply_convert_fusion
  807.8 13.4 convolution_add_fusion.4
  821.2 158.7 %all-gather.22.cloned.1.call-done = bf16[2048,4096]{1,0:T(8,128)(2,1)} async-done(((bf16[1024,4096]{1,0:T(8,128)(2,1)}), bf16[2048,4096]{1,0:T(8,128)(2,1)}) %all-gather.22.cloned.1.call-update) | async-done | bytes 16777232 | tf_op jit(solution)/shard_map/all_gather | solution.py:155
  980.0 13.7 multiply_reduce_fusion
  1000.0 3.2 convert_bitcast_fusion
  1009.6 3.0 multiply_add_fusion.1
  1014.3 3.3 convert_bitcast_fusion.1
  1017.7 3.2 convolution_convert_fusion.3
  1024.7 3.3 convert_bitcast_fusion.2
  1029.0 8.5 convolution_convert_fusion
  1038.7 8.2 convolution_convert_fusion.2
  1048.1 8.1 convolution_convert_fusion.1
  1057.7 4.2 copy.80
  1062.0 52.5 %reduce-scatter.23.cloned.1.call-done = bf16[1024,1024]{0,1:T(8,128)(2,1)} async-done(((bf16[2048,1024]{0,1:T(8,128)(2,1)}), bf16[1024,1024]{0,1:T(8,128)(2,1)}) %reduce-scatter.23.cloned.1.call-update) | async-done | bytes 2097168 | tf_op jit(solution)/shard_map/reduce_scatter | solution.py:262
  1114.4 4.2 copy.78
  1118.7 52.3 %reduce-scatter.27.cloned.1.call-done = bf16[512,2048]{1,0:T(8,128)(2,1)} async-done(((bf16[1024,2048]{1,0:T(8,128)(2,1)}), bf16[512,2048]{1,0:T(8,128)(2,1)}) %reduce-scatter.27.cloned.1.call-update) | async-done | bytes 2097168 | tf_op jit(solution)/shard_map/reduce_scatter | solution.py:268
  1171.0 4.1 convert_element_type.282
  1175.2 52.5 %reduce-scatter.21.cloned.1.call-done = bf16[1024,1024]{0,1:T(8,128)(2,1)} async-done(((bf16[2048,1024]{0,1:T(8,128)(2,1)}), bf16[1024,1024]{0,1:T(8,128)(2,1)}) %reduce-scatter.21.cloned.1.call-update) | async-done | bytes 2097168 | tf_op jit(solution)/shard_map/reduce_scatter | solution.py:259
  1227.7 4.1 copy.76
  1231.9 187.2 %reduce-scatter.39.cloned.1.call-done = bf16[2048,2048]{1,0:T(8,128)(2,1)} async-done(((bf16[4096,2048]{1,0:T(8,128)(2,1)}), bf16[2048,2048]{1,0:T(8,128)(2,1)}) %reduce-scatter.39.cloned.1.call-update) | async-done | bytes 8388624 | tf_op jit(solution)/shard_map/reduce_scatter | solution.py:181
  1419.1 11.8 convert_element_type.288
  1431.1 179.5 %reduce-scatter.31.cloned.1.call-done = bf16[1024,4096]{1,0:T(8,128)(2,1)} async-done(((bf16[2048,4096]{1,0:T(8,128)(2,1)}), bf16[1024,4096]{1,0:T(8,128)(2,1)}) %reduce-scatter.31.cloned.1.call-update) | async-done | bytes 8388624 | tf_op jit(solution)/shard_map/reduce_scatter | solution.py:175
  1610.6 11.9 convert_element_type.284
  1622.6 179.4 %reduce-scatter.35.cloned.1.call-done = bf16[1024,4096]{1,0:T(8,128)(2,1)} async-done(((bf16[2048,4096]{1,0:T(8,128)(2,1)}), bf16[1024,4096]{1,0:T(8,128)(2,1)}) %reduce-scatter.35.cloned.1.call-update) | async-done | bytes 8388624 | tf_op jit(solution)/shard_map/reduce_scatter | solution.py:178
  1802.0 11.6 convert_element_type.286
  1818.0 6.7 all-reduce.9
  1824.9 59.8 %all-reduce.8 = (f32[512]{0:T(512)S(1)}, f32[512]{0:T(512)S(1)}, f32[1024]{0:T(1024)S(1)}, f32[1024]{0:T(1024)S(1)}) all-reduce(f32[512]{0:T(512)S(1)} %dynamic-slice_convert_fusion.3, f32[512]{0:T(512)S(1)} %dynamic-slice_convert_fusion.2, ...), channel_id=17, replica_groups=mesh['shard'=2,'replica'=16] {'replica'}, use_global_device_ids=true, to_apply=%region_27.28.clone | all-reduce | flops 3072 | bytes 24576
  1887.0 3.9 convolution_add_fusion.2
  1895.9 59.8 %reduce-scatter.45.cloned.1.call-done = f32[64,1024]{1,0:T(8,128)} async-done(((f32[1024,1024]{1,0:T(8,128)}), f32[64,1024]{1,0:T(8,128)}) %reduce-scatter.45.cloned.1.call-update) | async-done | bytes 262160
  1955.7 76.1 %reduce-scatter.29.cloned.1.call-done = f32[32,2048]{1,0:T(8,128)} async-done(((f32[512,2048]{1,0:T(8,128)}), f32[32,2048]{1,0:T(8,128)}) %reduce-scatter.29.cloned.1.call-update) | async-done | bytes 262160 | tf_op jit(solution)/shard_map/reduce_scatter | solution.py:285
  2031.8 76.1 %reduce-scatter.43.cloned.1.call-done = f32[64,1024]{1,0:T(8,128)} async-done(((f32[1024,1024]{1,0:T(8,128)}), f32[64,1024]{1,0:T(8,128)}) %reduce-scatter.43.cloned.1.call-update) | async-done | bytes 262160
  2107.9 181.2 %reduce-scatter.41.cloned.1.call-done = f32[128,2048]{1,0:T(8,128)} async-done(((f32[2048,2048]{1,0:T(8,128)}), f32[128,2048]{1,0:T(8,128)}) %reduce-scatter.41.cloned.1.call-update) | async-done | bytes 1048592 | tf_op jit(solution)/shard_map/reduce_scatter | solution.py:191
  2289.1 181.0 %reduce-scatter.33.cloned.1.call-done = f32[64,4096]{1,0:T(8,128)} async-done(((f32[1024,4096]{1,0:T(8,128)}), f32[64,4096]{1,0:T(8,128)}) %reduce-scatter.33.cloned.1.call-update) | async-done | bytes 1048592 | tf_op jit(solution)/shard_map/reduce_scatter | solution.py:189
  2470.1 181.2 %reduce-scatter.37.cloned.1.call-done = f32[64,4096]{1,0:T(8,128)} async-done(((f32[1024,4096]{1,0:T(8,128)}), f32[64,4096]{1,0:T(8,128)}) %reduce-scatter.37.cloned.1.call-update) | async-done | bytes 1048592 | tf_op jit(solution)/shard_map/reduce_scatter | solution.py:190
  (212 shorter events, 47.5 us)
Async XLA Ops:
  7.2 337.4 %all-gather.14.cloned.1.call-start = ((), (), s32[]{:S(2)}) async-start(), calls=%async_computation.16 | async-start | bytes 6291456 | tf_op jit(solution)/shard_map/all_gather | solution.py:102
  7.9 340.7 %all-gather.12.cloned.1.call-start = ((), (), s32[]{:S(2)}) async-start(), calls=%async_computation.15 | async-start | bytes 6291456 | tf_op jit(solution)/shard_map/all_gather | solution.py:101
  8.7 346.1 %all-gather.10.cloned.1.call-start = ((), (), s32[]{:S(2)}) async-start(), calls=%async_computation.14 | async-start | bytes 6291456 | tf_op jit(solution)/shard_map/all_gather | solution.py:103
  9.4 369.6 %all-gather.16.cloned.1.call-start = ((), (), s32[]{:S(2)}) async-start(), calls=%async_computation.17 | async-start | bytes 6291456 | tf_op jit(solution)/shard_map/all_gather | solution.py:104
  10.0 569.3 %all-gather.18.cloned.1.call-start = ((), (), s32[]{:S(2)}) async-start(), calls=%async_computation.18 | async-start | bytes 25165824 | tf_op jit(solution)/shard_map/all_gather | solution.py:110
  10.6 769.0 %all-gather.20.cloned.1.call-start = ((), (), s32[]{:S(2)}) async-start(), calls=%async_computation.19 | async-start | bytes 25165824 | tf_op jit(solution)/shard_map/all_gather | solution.py:112
  11.1 3.9 copy-start.43
  11.2 319.5 %copy-start.44 = (bf16[512]{0:T(512)(128)(2,1)S(1)}, bf16[512]{0:T(512)(128)(2,1)}, u32[]{:S(2)}) copy-start(bf16[512]{0:T(512)(128)(2,1)} %param.22) | copy-start | bytes 3076
  11.2 323.9 %copy-start.41 = (bf16[1024]{0:T(1024)(128)(2,1)S(1)}, bf16[1024]{0:T(1024)(128)(2,1)}, u32[]{:S(2)}) copy-start(bf16[1024]{0:T(1024)(128)(2,1)} %param.24) | copy-start | bytes 6148
  11.2 328.5 %copy-start.42 = (bf16[1024]{0:T(1024)(128)(2,1)S(1)}, bf16[1024]{0:T(1024)(128)(2,1)}, u32[]{:S(2)}) copy-start(bf16[1024]{0:T(1024)(128)(2,1)} %param.25) | copy-start | bytes 6148
  11.2 333.4 %copy-start = (bf16[1,128,2048]{2,1,0:T(8,128)(2,1)S(1)}, bf16[1,128,2048]{2,1,0:T(8,128)(2,1)}, u32[]{:S(2)}) copy-start(bf16[1,128,2048]{2,1,0:T(8,128)(2,1)} %param.13) | copy-start | bytes 1572868
  11.2 968.8 %all-gather.22.cloned.1.call-start = ((), (), s32[]{:S(2)}) async-start(), calls=%async_computation.20 | async-start | bytes 25165824 | tf_op jit(solution)/shard_map/all_gather | solution.py:155
  11.9 1045.8 %reduce-scatter.25.cloned.1.call-start = ((), (), s32[]{:S(2)}) async-start(), calls=%async_computation.23 | async-start | bytes 6291456 | tf_op jit(solution)/shard_map/reduce_scatter | solution.py:265
  12.0 575.4 %collective-permute-start = (bf16[1024,4096]{1,0:T(8,128)(2,1)}, bf16[1024,4096]{1,0:T(8,128)(2,1)}, u32[]{:S(2)}, u32[]{:S(2)}) collective-permute-start(bf16[1024,4096]{1,0:T(8,128)(2,1)} %param.20), channel_id=1, source_target_pairs={{0,16},{16,0},{1,17},{17,1},{2,18},{18,2},{3,19},{19,3},{4,20},{20... | collective-permute-start | bytes 25165832 | tf_op jit(solution)/shard_map/ppermute | solution.py:17
  348.1 3.5 copy-start.37
  354.6 24.4 copy-start.5
  354.7 27.3 %copy-start.32 = (f32[8,128]{1,0:T(8,128)}, f32[8,128]{1,0:T(8,128)S(1)}, u32[]{:S(2)}) copy-start(f32[8,128]{1,0:T(8,128)S(1)} %log_add_fusion) | copy-start | bytes 12292
  357.7 21.3 copy-start.24
  358.0 229.4 %copy-start.22 = (bf16[8,128,128]{2,1,0:T(8,128)(2,1)}, bf16[8,128,128]{2,1,0:T(8,128)(2,1)S(1)}, u32[]{:S(2)}) copy-start(bf16[8,128,128]{2,1,0:T(8,128)(2,1)S(1)} %convolution_convert_fusion.5) | copy-start | bytes 786436
  779.5 8.6 copy-start.14
  788.1 19.6 copy-start.47
  788.1 205.6 %copy-start.39 = (f32[128]{0:T(128)}, f32[128]{0:T(128)S(1)}, u32[]{:S(2)}) copy-start(f32[128]{0:T(128)S(1)} %get-tuple-element.84) | copy-start | bytes 1540
  789.1 18.7 copy-start.49
  993.7 3.5 copy-start.3
  1003.2 111.2 %reduce-scatter.23.cloned.1.call-start = ((), (), s32[]{:S(2)}) async-start(), calls=%async_computation.22 | async-start | bytes 6291456 | tf_op jit(solution)/shard_map/reduce_scatter | solution.py:262
  1007.0 6.2 copy-start.10
  1009.6 3.5 copy-start.38
  1009.6 3.7 copy-start.46
  1014.3 3.4 copy-start.13
  1014.3 3.4 copy-start.23
  1017.6 153.4 %reduce-scatter.27.cloned.1.call-start = ((), (), s32[]{:S(2)}) async-start(), calls=%async_computation.24 | async-start | bytes 6291456 | tf_op jit(solution)/shard_map/reduce_scatter | solution.py:268
  1021.0 206.7 %reduce-scatter.21.cloned.1.call-start = ((), (), s32[]{:S(2)}) async-start(), calls=%async_computation.21 | async-start | bytes 6291456 | tf_op jit(solution)/shard_map/reduce_scatter | solution.py:259
  1028.0 391.1 %reduce-scatter.39.cloned.1.call-start = ((), (), s32[]{:S(2)}) async-start(), calls=%async_computation.30 | async-start | bytes 25165824 | tf_op jit(solution)/shard_map/reduce_scatter | solution.py:181
  1037.5 573.1 %reduce-scatter.31.cloned.1.call-start = ((), (), s32[]{:S(2)}) async-start(), calls=%async_computation.26 | async-start | bytes 25165824 | tf_op jit(solution)/shard_map/reduce_scatter | solution.py:175
  1046.9 755.1 %reduce-scatter.35.cloned.1.call-start = ((), (), s32[]{:S(2)}) async-start(), calls=%async_computation.28 | async-start | bytes 25165824 | tf_op jit(solution)/shard_map/reduce_scatter | solution.py:178
  1056.2 839.7 %reduce-scatter.47.cloned.1.call-start = ((), (), s32[]{:S(2)}) async-start(), calls=%async_computation.34 | async-start | bytes 4456448
  1061.9 893.8 %reduce-scatter.45.cloned.1.call-start = ((), (), s32[]{:S(2)}) async-start(), calls=%async_computation.33 | async-start | bytes 4456448
  1118.6 913.2 %reduce-scatter.29.cloned.1.call-start = ((), (), s32[]{:S(2)}) async-start(), calls=%async_computation.25 | async-start | bytes 4456448 | tf_op jit(solution)/shard_map/reduce_scatter | solution.py:285
  1175.1 932.8 %reduce-scatter.43.cloned.1.call-start = ((), (), s32[]{:S(2)}) async-start(), calls=%async_computation.32 | async-start | bytes 4456448
  1231.9 1057.2 %reduce-scatter.41.cloned.1.call-start = ((), (), s32[]{:S(2)}) async-start(), calls=%async_computation.31 | async-start | bytes 17825792 | tf_op jit(solution)/shard_map/reduce_scatter | solution.py:191
  1430.9 1039.2 %reduce-scatter.33.cloned.1.call-start = ((), (), s32[]{:S(2)}) async-start(), calls=%async_computation.27 | async-start | bytes 17825792 | tf_op jit(solution)/shard_map/reduce_scatter | solution.py:189
  1622.5 1028.7 %reduce-scatter.37.cloned.1.call-start = ((), (), s32[]{:S(2)}) async-start(), calls=%async_computation.29 | async-start | bytes 17825792 | tf_op jit(solution)/shard_map/reduce_scatter | solution.py:190
  1813.6 4.4 copy-start.33
  1813.6 4.4 copy-start.34
  1813.6 73.4 %copy-start.4 = (f32[128,2048]{1,0:T(8,128)S(1)}, f32[128,2048]{1,0:T(8,128)}, u32[]{:S(2)}) copy-start(f32[128,2048]{1,0:T(8,128)} %get-tuple-element.97) | copy-start | bytes 3145732
  1813.6 73.4 %copy-start.21 = (bf16[128,1024]{1,0:T(8,128)(2,1)S(1)}, bf16[128,1024]{1,0:T(8,128)(2,1)}, u32[]{:S(2)}) copy-start(bf16[128,1024]{1,0:T(8,128)(2,1)} %copy-done.20) | copy-start | bytes 786436
  1813.6 77.3 %copy-start.19 = (bf16[128,1024]{1,0:T(8,128)(2,1)S(1)}, bf16[128,1024]{1,0:T(8,128)(2,1)}, u32[]{:S(2)}) copy-start(bf16[128,1024]{1,0:T(8,128)(2,1)} %copy-done.18) | copy-start | bytes 786436
  1884.7 6.2 copy-start.1
  (27 other events, 47.9 us)
Sparse Core Ops, SparseCore 0:
  9.5 104.4 all-gather.13
  115.6 101.7 all-gather.11
  218.9 101.7 all-gather.9
  322.1 56.8 all-gather.15
  380.4 198.8 all-gather.17
  580.7 198.8 all-gather.19
  781.1 198.8 all-gather.21
  1003.3 54.3 reduce-scatter.24
  1060.0 54.3 reduce-scatter.22
  1116.6 54.3 reduce-scatter.26
  1173.3 54.3 reduce-scatter.20
  1229.9 189.1 reduce-scatter.38
  1421.4 189.1 reduce-scatter.30
  1612.8 189.1 reduce-scatter.34
  1806.3 73.4 reduce-scatter.46
  1884.1 71.5 reduce-scatter.44
  1960.0 71.8 reduce-scatter.28
  2036.1 71.7 reduce-scatter.42
  2112.6 176.4 reduce-scatter.40
  2293.6 176.4 reduce-scatter.32
  2474.7 176.4 reduce-scatter.36
